TPU v7x, 256 devices: a 8x8x2 block of a 8x8x16 slice. The times are simulated.
256 devices in a mesh: scen: 2 (over z), gx: 128 (over y, x, core).
Axes of the slice: x: 8, y: 8, z: 2, core: 2. Of those that a mesh axis runs over, the one named last changes fastest.
The devices are a block of a 8x8x16 slice.
Arguments:
- populations: float32 [54, 128, 4, 8, 256], P('scen', 'gx'), parts along dimension 0, may hold values from 0.15 to 2
- cell_kind: int32 [128, 4, 8, 512], P('gx', None, None, 'scen'), parts along dimension 3, may hold values from 0 to 4, as said below
- profile: int32 [128, 4, 8, 512], P('gx', None, None, 'scen'), parts along dimension 3, may hold values from 0 to 7
- vent_table: float32 [16, 3], P('scen'), parts along dimension 0, may hold values from -0.08 to 0.08
- rates: float32 [27], replicated, may hold values from 1 to 1.9
Outputs:
- advanced: float32 [54, 128, 4, 8, 256], P('scen', 'gx'), parts along dimension 0
There are 2 independent parts, one for each index of `scen`. A program takes and returns all parts, laid end to end along the dimension named above; an argument that names none is the same for every part. Nothing has to cross between parts.
Inputs may be any that keep to these rules, and one draw needn't show every extreme that they name: `cell_kind`: 0 fluid, 1 wall, 2 vent, 3 inflow, 4 outflow.
All inputs are finite; a program needn't handle non-finite values.
Results may differ from a plain program's by a relative error of at most 0.0003.
Values sent between devices are 32-bit elements; how exact they have to be, the bound alone decides.
A program may use at most 64 MiB of HBM per device.

v0:
```python
import jax
import jax.numpy as jnp
from jax import lax
from jax.experimental import pallas as pl
from jax.experimental.pallas import tpu as pltpu
from jax.sharding import PartitionSpec as P

PY = 8
STEPS = 3
BIG = 1e30
MESH = pl.DeviceIdType.MESH

RIGHT, LEFT, UP, DOWN, RIGHT_UP, LEFT_DOWN, RIGHT_DOWN, LEFT_UP = range(8)
OFFSETS = (PY, -PY, 1, -1, PY + 1, -PY - 1, PY - 1, -PY + 1)


def direction(a, b, e):
    return 9 * (a + 1) + 3 * (b + 1) + (e + 1)


def digits(k):
    return (k // 9, k // 3 % 3, k % 3)


def forward(values):
    values = list(values)
    for stride in (1, 3, 9):
        for k in range(27):
            if k // stride % 3 == 0:
                low, mid, high = (values[k], values[k + stride], values[k + 2 * stride])
                both = low + high
                values[k] = both + 4.0 * mid
                values[k + stride] = high - low
                values[k + 2 * stride] = both
    return values


def backward(values):
    values = list(values)
    for stride in (9, 3, 1):
        for k in range(27):
            if k // stride % 3 == 0:
                zero, one, two = (values[k], values[k + stride], values[k + 2 * stride])
                values[k] = two - one
                values[k + stride] = zero - 0.5 * two
                values[k + 2 * stride] = two + one
    return values


def equilibrium_moments(density, velocity):
    share = [density]
    for _ in range(3):
        share.append(share[-1] * (1.0 / 3.0))
    triple = [3.0 * component * component for component in velocity]
    result = []
    for k in range(27):
        powers = digits(k)
        ones = [axis for axis in range(3) if powers[axis] == 1]
        twos = [axis for axis in range(3) if powers[axis] == 2]
        scale = share[len(twos)]
        if len(ones) == 0:
            shape = None
            for axis in twos:
                shape = 1.0 + triple[axis] if shape is None else shape + triple[axis]
            result.append(scale if shape is None else scale * shape)
        elif len(ones) == 3:
            result.append(None)
        else:
            shape = velocity[ones[0]]
            for axis in ones[1:]:
                shape = shape * velocity[axis]
            result.append(scale * shape)
    return result


def equilibrium(velocity):
    square = velocity[0] * velocity[0] + velocity[1] * velocity[1] + velocity[2] * velocity[2]
    base = 1.0 - 1.5 * square
    result = [None] * 27
    result[13] = base
    for k in range(13):
        projected = None
        for axis, digit in enumerate(digits(k)):
            if digit != 1:
                term = velocity[axis] if digit == 2 else -velocity[axis]
                projected = term if projected is None else projected + term
        even = base + 4.5 * projected * projected
        odd = 3.0 * projected
        result[k] = even + odd
        result[26 - k] = even - odd
    return result


def shifted(main, row, b, e, lane_count):
    if b != 0:
        count = main.shape[0]
        place = lax.broadcasted_iota(jnp.int32, main.shape, 0)
        moved = pltpu.roll(main, 1 if b == 1 else count - 1, 0)
        main = jnp.where(place == (0 if b == 1 else count - 1), row, moved)
    if e != 0:
        main = pltpu.roll(main, 1 if e == 1 else lane_count - 1, 1)
    return main


def kernel(
    populations, cell_kind, profile, vent_table, rates, out,
    start, collided, passed, walls, inlet, coef, kinds, profiles,
    rim_kinds, rim_profiles, fields, rim_fields,
    get_x, put_y, get_y, put_d, get_d,
    put_kx, get_kx, put_ky, get_ky, put_kd, get_kd,
    load_sem, out_sem, send_sem, recv_sem,
):
    me = lax.axis_index("gx")
    count = lax.axis_size("gx")
    depth, rows, cells = collided.shape[2], collided.shape[3], collided.shape[4]
    last = depth - 1
    half = cells // 2
    row_place = lax.rem(me + PY // 2, PY)
    targets = [lax.rem(me + count + offset, count) for offset in OFFSETS]

    barrier = pltpu.get_barrier_semaphore()
    for target in targets:
        pl.semaphore_signal(barrier, inc=1, device_id={"gx": target}, device_id_type=MESH)

    order = (0, last) + tuple(range(1, last))
    loads = {}
    for x in order:
        loads[x] = pltpu.make_async_copy(populations.at[:, 0, x], start.at[:, x], load_sem.at[x])
        loads[x].start()
    kind_load = pltpu.make_async_copy(cell_kind.at[0], kinds, load_sem.at[depth])
    profile_load = pltpu.make_async_copy(profile.at[0], profiles, load_sem.at[depth + 1])
    kind_load.start()
    profile_load.start()

    def remote(source, target_ref, slot, message):
        return pltpu.make_async_remote_copy(
            src_ref=source,
            dst_ref=target_ref,
            send_sem=send_sem.at[slot, message],
            recv_sem=recv_sem.at[slot, message],
            device_id={"gx": targets[message]},
            device_id_type=MESH,
        )

    def message(step, which):
        if which == RIGHT:
            return remote(collided.at[step, pl.ds(18, 9), last], get_x.at[step, 0], step, which)
        if which == LEFT:
            return remote(collided.at[step, pl.ds(0, 9), 0], get_x.at[step, 1], step, which)
        if which in (UP, DOWN):
            return remote(put_y.at[step, which - UP], get_y.at[step, which - UP], step, which)
        return remote(put_d.at[step, which - RIGHT_UP], get_d.at[step, which - RIGHT_UP], step, which)

    def kind_message(which):
        if which in (RIGHT, LEFT):
            return remote(put_kx.at[which], get_kx.at[which], STEPS, which)
        if which in (UP, DOWN):
            return remote(put_ky.at[which - UP], get_ky.at[which - UP], STEPS, which)
        return remote(put_kd.at[which - RIGHT_UP], get_kd.at[which - RIGHT_UP], STEPS, which)

    for k in range(27):
        scale = 1.0
        for digit in digits(k):
            scale = scale * (0.25 if digit == 0 else 0.5)
        rate = rates[k]
        coef[2 * k] = jnp.full((rows, half), scale * (1.0 - rate), jnp.float32)
        coef[2 * k + 1] = jnp.full((rows, half), scale * rate, jnp.float32)

    def relaxed(moments, target):
        result = []
        for k in range(27):
            value = coef[2 * k] * moments[k]
            if target[k] is not None:
                value = value + coef[2 * k + 1] * target[k]
            result.append(value)
        return backward(result)

    def collide_first(x, lanes):
        moments = forward([start[k, x, :, lanes] for k in range(27)])
        density = moments[0]
        velocity = [moments[k] / density for k in (9, 3, 1)]
        result = relaxed(moments, equilibrium_moments(density, velocity))
        for k in range(27):
            collided[0, k, x, :, lanes] = result[k]

    def cell_state(step, x, lanes):
        values = [
            collided[step, k, x, :, lanes] if k == 13 else passed[k, x, :, lanes]
            for k in range(27)
        ]
        moments = forward(values)
        velocity = [moments[k] / moments[0] for k in (9, 3, 1)]
        return (values, moments, velocity, kinds[x, :, lanes])

    def collide_next(step, x, lanes):
        values, moments, velocity, kind = cell_state(step, x, lanes)
        fluid = kind == 0
        moving = fluid | (kind == 4)
        velocity = [
            jnp.where(moving, velocity[axis], inlet[axis, x, :, lanes]) for axis in range(3)
        ]
        density = jnp.where(fluid, moments[0], 216.0)
        target = equilibrium_moments(density, velocity)
        moments = [
            jnp.where(fluid, moments[k], 0.0 if target[k] is None else target[k])
            for k in range(27)
        ]
        result = relaxed(moments, target)
        for k in range(27):
            collided[step + 1, k, x, :, lanes] = result[k]

    def finish(step, x, lanes):
        values, moments, velocity, kind = cell_state(step, x, lanes)
        fluid = kind == 0
        velocity = [
            jnp.where(kind == 4, velocity[axis], inlet[axis, x, :, lanes]) for axis in range(3)
        ]
        forced = equilibrium(velocity)
        for k in range(27):
            start[k, x, :, lanes] = jnp.where(fluid, values[k], forced[k])

    def by_halves(work, planes):
        def body(index, carry):
            plane = planes[0] + index // 2
            lanes = pl.ds(pl.multiple_of(index % 2 * half, half), half)
            work(plane, lanes)
            return carry

        lax.fori_loop(0, 2 * len(planes), body, 0)

    def stage_diagonal(step, which):
        a = 1 if which in (RIGHT_UP, RIGHT_DOWN) else -1
        b = 1 if which in (RIGHT_UP, LEFT_UP) else -1
        x = last if a == 1 else 0
        y = rows - 1 if b == 1 else 0
        for e in range(3):
            row = collided[step, direction(a, b, e - 1), x, pl.ds(y, 1), :]
            put_d[step, which - RIGHT_UP, pl.ds(2 * e, 1), :] = row[:, :half]
            put_d[step, which - RIGHT_UP, pl.ds(2 * e + 1, 1), :] = row[:, half:]

    def stage_rows(step):
        for which, b, y in ((0, 1, rows - 1), (1, -1, 0)):
            for pair in range(9):
                k = direction(pair // 3 - 1, b, pair % 3 - 1)
                for x in range(depth):
                    put_y[step, which, pl.ds(pair * depth + x, 1), :] = collided[
                        step, k, x, pl.ds(y, 1), :
                    ]

    def passed_plane(step, x):
        for k in range(27):
            if k == 13:
                continue
            a, b, e = (digit - 1 for digit in digits(k))
            origin = x - a
            row = None
            if origin < 0 or origin > last:
                side = 0 if a == 1 else 1
                main = get_x[step, side, 3 * (b + 1) + (e + 1)]
                if b != 0:
                    if a == 1:
                        which = RIGHT_UP if b == 1 else RIGHT_DOWN
                    else:
                        which = LEFT_UP if b == 1 else LEFT_DOWN
                    corner = get_d.at[step, which - RIGHT_UP]
                    row = jnp.concatenate(
                        [corner[pl.ds(2 * e + 2, 1), :], corner[pl.ds(2 * e + 3, 1), :]], axis=1
                    )
            else:
                main = collided[step, k, origin]
                if b != 0:
                    place = (3 * (a + 1) + (e + 1)) * depth + origin
                    row = get_y[step, 0 if b == 1 else 1, pl.ds(place, 1), :]
            source = shifted(main, row, b, e, cells)
            wall = walls[k, x]
            passed[k, x] = jnp.where(wall > 0.5 * BIG, source, collided[step, 26 - k, x] + wall)

    def field_values(kind, index):
        velocity = [jnp.zeros(kind.shape, jnp.float32) for _ in range(3)]
        for entry in range(vent_table.shape[0]):
            chosen = index == entry
            for axis in range(3):
                velocity[axis] = jnp.where(chosen, vent_table[entry, axis], velocity[axis])
        is_open = (kind == 0) | (kind >= 3)
        vent = kind == 2
        result = [jnp.where(is_open, BIG, 0.0)]
        for axis in range(3):
            result.append(jnp.where(vent, velocity[axis], 0.0))
        return result, velocity

    def prepare_walls():
        for plane in range(depth + 2):
            if plane == 0:
                kind, index = get_kx[RIGHT, 0], get_kx[RIGHT, 1]
            elif plane == depth + 1:
                kind, index = get_kx[LEFT, 0], get_kx[LEFT, 1]
            else:
                kind, index = kinds[plane - 1], profiles[plane - 1]
            values, velocity = field_values(kind, index)
            for field in range(4):
                fields[field, plane] = values[field]
            if 1 <= plane <= depth:
                for axis in range(3):
                    inlet[axis, plane - 1] = jnp.where(kind == 3, velocity[axis], 0.0)
        for side, b in ((0, 1), (1, -1)):
            low = (RIGHT_UP if b == 1 else RIGHT_DOWN) - RIGHT_UP
            high = (LEFT_UP if b == 1 else LEFT_DOWN) - RIGHT_UP
            for target, shift in ((rim_kinds, 0), (rim_profiles, 1)):
                target[side] = jnp.zeros((rows, cells), jnp.int32)
                target[side, pl.ds(1, depth), :] = get_ky[side, pl.ds(shift * depth, depth), :]
                for row, corner in ((0, low), (depth + 1, high)):
                    for part in range(2):
                        target[side, pl.ds(row, 1), pl.ds(part * half, half)] = get_kd[
                            corner, pl.ds(2 * shift + part, 1), :
                        ]
            outside = row_place == (0 if b == 1 else PY - 1)
            kind = jnp.where(outside, 1, rim_kinds[side])
            values, _ = field_values(kind, rim_profiles[side])
            for field in range(4):
                rim_fields[side, field] = values[field]
        lane = lax.broadcasted_iota(jnp.int32, (rows, cells), 1)
        for plane in range(depth + 2):
            for b in (-1, 0, 1):
                for e in (-1, 0, 1):
                    moved = []
                    for field in range(4):
                        row = None
                        if b != 0:
                            row = rim_fields[0 if b == 1 else 1, field, pl.ds(plane, 1), :]
                        value = shifted(fields[field, plane], row, b, e, cells)
                        if e != 0:
                            value = jnp.where(lane == (0 if e == 1 else cells - 1), 0.0, value)
                        moved.append(value)
                    cross = moved[0]
                    if b != 0:
                        cross = cross + (6.0 * b) * moved[2]
                    if e != 0:
                        cross = cross + (6.0 * e) * moved[3]
                    for a in (-1, 0, 1):
                        x = plane - 1 + a
                        k = direction(a, b, e)
                        if 0 <= x <= last and k != 13:
                            walls[k, x] = cross if a == 0 else cross + (6.0 * a) * moved[1]

    for x in order:
        loads[x].wait()
        by_halves(collide_first, (x,))
    for which in range(RIGHT_UP, LEFT_UP + 1):
        stage_diagonal(0, which)
    stage_rows(0)
    kind_load.wait()
    profile_load.wait()
    for which, x in ((RIGHT, last), (LEFT, 0)):
        put_kx[which, 0] = kinds[x]
        put_kx[which, 1] = profiles[x]
    for side, y in ((0, rows - 1), (1, 0)):
        for x in range(depth):
            put_ky[side, pl.ds(x, 1), :] = kinds[x, pl.ds(y, 1), :]
            put_ky[side, pl.ds(depth + x, 1), :] = profiles[x, pl.ds(y, 1), :]
    for which in range(RIGHT_UP, LEFT_UP + 1):
        x = last if which in (RIGHT_UP, RIGHT_DOWN) else 0
        y = rows - 1 if which in (RIGHT_UP, LEFT_UP) else 0
        for shift, source in ((0, kinds), (1, profiles)):
            row = source[x, pl.ds(y, 1), :]
            put_kd[which - RIGHT_UP, pl.ds(2 * shift, 1), :] = row[:, :half]
            put_kd[which - RIGHT_UP, pl.ds(2 * shift + 1, 1), :] = row[:, half:]

    pl.semaphore_wait(barrier, len(targets))
    for which in range(8):
        message(0, which).start()
    for which in range(8):
        kind_message(which).start()

    outs = []
    for step in range(STEPS):
        final = step == STEPS - 1
        work = finish if final else collide_next

        def advance(planes):
            for x in planes:
                passed_plane(step, x)
            by_halves(lambda x, lanes: work(step, x, lanes), planes)
            if final:
                for x in planes:
                    copy = pltpu.make_async_copy(start.at[:, x], out.at[:, 0, x], out_sem.at[x])
                    copy.start()
                    outs.append(copy)

        if step == 0:
            for which in range(8):
                kind_message(which).wait_recv()
            prepare_walls()
        for which in (UP, DOWN):
            message(step, which).wait_recv()
        advance(tuple(range(1, last)))
        for x, needed, sent in (
            (0, (RIGHT, RIGHT_UP, RIGHT_DOWN), (LEFT, LEFT_DOWN, LEFT_UP)),
            (last, (LEFT, LEFT_DOWN, LEFT_UP), (RIGHT, RIGHT_UP, RIGHT_DOWN)),
        ):
            for which in needed:
                message(step, which).wait_recv()
            advance((x,))
            if not final:
                message(step + 1, sent[0]).start()
                for which in sent[1:]:
                    stage_diagonal(step + 1, which)
                    message(step + 1, which).start()
        if not final:
            stage_rows(step + 1)
            for which in (UP, DOWN):
                message(step + 1, which).start()

    for step in range(STEPS):
        for which in range(8):
            message(step, which).wait_send()
    for which in range(8):
        kind_message(which).wait_send()
    for copy in outs:
        copy.wait()


def local(populations, cell_kind, profile, vent_table, rates):
    _, _, depth, rows, cells = populations.shape
    half = cells // 2
    strip = (9 * depth + 7) // 8 * 8
    f32, i32 = jnp.float32, jnp.int32
    anywhere = pl.BlockSpec(memory_space=pl.ANY)
    scalar = pl.BlockSpec(memory_space=pltpu.SMEM)
    return pl.pallas_call(
        kernel,
        out_shape=jax.ShapeDtypeStruct(populations.shape, f32),
        in_specs=[anywhere, anywhere, anywhere, scalar, scalar],
        out_specs=anywhere,
        scratch_shapes=[
            pltpu.VMEM((27, depth, rows, cells), f32),
            pltpu.VMEM((STEPS, 27, depth, rows, cells), f32),
            pltpu.VMEM((27, depth, rows, cells), f32),
            pltpu.VMEM((27, depth, rows, cells), f32),
            pltpu.VMEM((3, depth, rows, cells), f32),
            pltpu.VMEM((54, rows, half), f32),
            pltpu.VMEM((depth, rows, cells), i32),
            pltpu.VMEM((depth, rows, cells), i32),
            pltpu.VMEM((2, rows, cells), i32),
            pltpu.VMEM((2, rows, cells), i32),
            pltpu.VMEM((4, depth + 2, rows, cells), f32),
            pltpu.VMEM((2, 4, rows, cells), f32),
            pltpu.VMEM((STEPS, 2, 9, rows, cells), f32),
            pltpu.VMEM((STEPS, 2, strip, cells), f32),
            pltpu.VMEM((STEPS, 2, strip, cells), f32),
            pltpu.VMEM((STEPS, 4, 8, half), f32),
            pltpu.VMEM((STEPS, 4, 8, half), f32),
            pltpu.VMEM((2, 2, rows, cells), i32),
            pltpu.VMEM((2, 2, rows, cells), i32),
            pltpu.VMEM((2, 2 * depth, cells), i32),
            pltpu.VMEM((2, 2 * depth, cells), i32),
            pltpu.VMEM((4, 8, half), i32),
            pltpu.VMEM((4, 8, half), i32),
            pltpu.SemaphoreType.DMA((depth + 2,)),
            pltpu.SemaphoreType.DMA((depth,)),
            pltpu.SemaphoreType.DMA((STEPS + 1, 8)),
            pltpu.SemaphoreType.DMA((STEPS + 1, 8)),
        ],
        compiler_params=pltpu.CompilerParams(collective_id=0, has_side_effects=True),
        name="lattice_steps",
    )(populations, cell_kind, profile, vent_table, rates)


def solution(mesh):
    return jax.shard_map(
        local,
        mesh=mesh,
        in_specs=(
            P("scen", "gx", None, None, None),
            P("gx", None, None, "scen"),
            P("gx", None, None, "scen"),
            P("scen", None),
            P(),
        ),
        out_specs=P("scen", "gx", None, None, None),
        check_vma=False,
    )
```

profile of v0, /device:TPU:513, one launch (start us, length us, event | category | flops | bytes accessed | tf_op | source)
XLA Modules:
  0.0 64.7 jit_solution(15803609713171782476)
XLA Ops:
  0.0 1.3 %copy.6.vent_table = f32[8,3]{1,0:T(8,128)} copy(f32[8,3]{0,1:T(4,128)} %param.8) | data formatting | bytes 192 | tf_op args[3]
  1.3 61.1 %lattice_steps.1 = f32[27,1,4,8,256]{4,3,2,1,0:T(8,128)} custom-call(f32[27,1,4,8,256]{4,3,2,1,0:T(8,128)} %populations.1, s32[1,4,8,256]{3,2,1,0:T(8,128)} %cell_kind.1, s32[1,4,8,256]{3,2,1,0:T(8,128)} %profile.1, f32[8,3]{1,0:T(8,128)} %copy.6.vent_table, f32[27]{0:T(128)} %rates.1), custom_call_target="tpu_custom_call" | custom-call | tf_op jit(solution)/shard_map/lattice_steps/pallas_call | solution.py:429
  62.5 2.2 %copy.8 = f32[27,1,4,8,256]{4,3,2,1,0:T(8,128)} copy(f32[27,1,4,8,256]{4,3,2,1,0:T(8,128)} %lattice_steps.1) | data formatting | bytes 1769472
where the time goes:
time: 64.9 us; the launch traced here: 64.7 us
  Pallas kernels  61.1 us (94%)
  local copies, waits for them, and re-layouts  3.52 us (5%)
    pallas_call x1, Pallas kernels, local(): pl.pallas_call(kernel, out_shape=jax.ShapeDtypeStruct(populations.shape,...  61.1 us
    unnamed x2, local copies, waits for them, and re-layouts  3.52 us

commit v1 on v0

--- a/solution.py
+++ b/solution.py
@@ -10,8 +10,7 @@
 BIG = 1e30
 MESH = pl.DeviceIdType.MESH
 
-RIGHT, LEFT, UP, DOWN, RIGHT_UP, LEFT_DOWN, RIGHT_DOWN, LEFT_UP = range(8)
-OFFSETS = (PY, -PY, 1, -1, PY + 1, -PY - 1, PY - 1, -PY + 1)
+ACROSS, CORNER, ALONG, ROW = 0, 2, 6, 12
 
 
 def direction(a, b, e):
@@ -116,11 +115,24 @@
     last = depth - 1
     half = cells // 2
     row_place = lax.rem(me + PY // 2, PY)
-    targets = [lax.rem(me + count + offset, count) for offset in OFFSETS]
+    far_right = lax.rem(me // PY, 2) == 1
+    has_row = (row_place != PY - 1, row_place != 0)
+
+    def device(side, turn):
+        place = me + count
+        if side is not None:
+            place = place + (PY - 2 * PY * side)
+        if turn is not None:
+            place = place + (1 - 2 * turn)
+        return lax.rem(place, count)
 
     barrier = pltpu.get_barrier_semaphore()
-    for target in targets:
-        pl.semaphore_signal(barrier, inc=1, device_id={"gx": target}, device_id_type=MESH)
+    for side in (None, 0, 1):
+        for turn in (None, 0, 1):
+            if side is not None or turn is not None:
+                pl.semaphore_signal(
+                    barrier, inc=1, device_id={"gx": device(side, turn)}, device_id_type=MESH
+                )
 
     order = (0, last) + tuple(range(1, last))
     loads = {}
@@ -132,31 +144,65 @@
     kind_load.start()
     profile_load.start()
 
-    def remote(source, target_ref, slot, message):
+    def remote(source, target_ref, slot, place, side, turn):
         return pltpu.make_async_remote_copy(
             src_ref=source,
             dst_ref=target_ref,
-            send_sem=send_sem.at[slot, message],
-            recv_sem=recv_sem.at[slot, message],
-            device_id={"gx": targets[message]},
+            send_sem=send_sem.at[slot, place],
+            recv_sem=recv_sem.at[slot, place],
+            device_id={"gx": device(side, turn)},
             device_id_type=MESH,
         )
 
-    def message(step, which):
-        if which == RIGHT:
-            return remote(collided.at[step, pl.ds(18, 9), last], get_x.at[step, 0], step, which)
-        if which == LEFT:
-            return remote(collided.at[step, pl.ds(0, 9), 0], get_x.at[step, 1], step, which)
-        if which in (UP, DOWN):
-            return remote(put_y.at[step, which - UP], get_y.at[step, which - UP], step, which)
-        return remote(put_d.at[step, which - RIGHT_UP], get_d.at[step, which - RIGHT_UP], step, which)
-
-    def kind_message(which):
-        if which in (RIGHT, LEFT):
-            return remote(put_kx.at[which], get_kx.at[which], STEPS, which)
-        if which in (UP, DOWN):
-            return remote(put_ky.at[which - UP], get_ky.at[which - UP], STEPS, which)
-        return remote(put_kd.at[which - RIGHT_UP], get_kd.at[which - RIGHT_UP], STEPS, which)
+    def across(step, side):
+        source = collided.at[step, pl.ds(18 - 18 * side, 9), last - last * side]
+        return remote(source, get_x.at[step, side], step, ACROSS + side, side, None)
+
+    def corner(step, side, turn):
+        place = 2 * side + turn
+        return remote(
+            put_d.at[step, place], get_d.at[step, place], step, CORNER + place, side, turn
+        )
+
+    def along(step, turn, first, size, place):
+        part = pl.ds(first, size)
+        return remote(
+            put_y.at[step, turn, part], get_y.at[step, turn, part], step,
+            ALONG + 3 * turn + place, None, turn,
+        )
+
+    def along_edge(step, turn, side):
+        return along(step, turn, 9 * last - (9 * last - 3) * side, 6, 2 - 2 * side)
+
+    def along_middle(step, turn):
+        return along(step, turn, 9, 9 * (last - 1), 1)
+
+    def kind_across(side):
+        return remote(put_kx.at[side], get_kx.at[side], STEPS, ACROSS + side, side, None)
+
+    def kind_corner(side, turn):
+        place = 2 * side + turn
+        return remote(
+            put_kd.at[place], get_kd.at[place], STEPS, CORNER + place, side, turn
+        )
+
+    def kind_along(turn):
+        return remote(put_ky.at[turn], get_ky.at[turn], STEPS, ALONG + turn, None, turn)
+
+    def go(copy, turn):
+        @pl.when(has_row[turn])
+        def _():
+            copy().start()
+
+    def sent(copy, turn):
+        @pl.when(has_row[turn])
+        def _():
+            copy().wait_send()
+
+    def came(copy, turn):
+        @pl.when(has_row[1 - turn])
+        def _():
+            copy().wait_recv()
 
     for k in range(27):
         scale = 1.0
@@ -219,68 +265,87 @@
         for k in range(27):
             start[k, x, :, lanes] = jnp.where(fluid, values[k], forced[k])
 
-    def by_halves(work, planes):
+    def by_halves(work, first, planes):
         def body(index, carry):
-            plane = planes[0] + index // 2
+            plane = first + index // 2
             lanes = pl.ds(pl.multiple_of(index % 2 * half, half), half)
             work(plane, lanes)
             return carry
 
-        lax.fori_loop(0, 2 * len(planes), body, 0)
-
-    def stage_diagonal(step, which):
-        a = 1 if which in (RIGHT_UP, RIGHT_DOWN) else -1
-        b = 1 if which in (RIGHT_UP, LEFT_UP) else -1
-        x = last if a == 1 else 0
-        y = rows - 1 if b == 1 else 0
-        for e in range(3):
-            row = collided[step, direction(a, b, e - 1), x, pl.ds(y, 1), :]
-            put_d[step, which - RIGHT_UP, pl.ds(2 * e, 1), :] = row[:, :half]
-            put_d[step, which - RIGHT_UP, pl.ds(2 * e + 1, 1), :] = row[:, half:]
-
-    def stage_rows(step):
-        for which, b, y in ((0, 1, rows - 1), (1, -1, 0)):
-            for pair in range(9):
-                k = direction(pair // 3 - 1, b, pair % 3 - 1)
-                for x in range(depth):
-                    put_y[step, which, pl.ds(pair * depth + x, 1), :] = collided[
-                        step, k, x, pl.ds(y, 1), :
-                    ]
-
-    def passed_plane(step, x):
+        lax.fori_loop(0, 2 * planes, body, 0)
+
+    def stage_corners(step, side):
+        x = last - last * side
+        for turn in range(2):
+            y = rows - 1 if turn == 0 else 0
+            for e in range(3):
+                k = 18 - 18 * side + (6 - 6 * turn) + e
+                put_d[step, 2 * side + turn, e] = collided[step, k, x, pl.ds(y, 1), :]
+
+    def stage_rows(step, x, pairs):
+        for turn in range(2):
+            y = rows - 1 if turn == 0 else 0
+            for pair in pairs:
+                k = 9 * (pair // 3) + (6 - 6 * turn) + pair % 3
+                put_y[step, turn, 9 * x + pair] = collided[step, k, x, pl.ds(y, 1), :]
+
+    def stage_edge(step, side):
+        x = last - last * side
+        for turn in range(2):
+            y = rows - 1 if turn == 0 else 0
+            for pair in range(6):
+                k = 9 * (pair // 3) + 9 * side + (6 - 6 * turn) + pair % 3
+                row = 9 * last - (9 * last - 3) * side + pair
+                put_y[step, turn, row] = collided[step, k, x, pl.ds(y, 1), :]
+
+    def passed_on(step, k, x, opposite, main, row, b, e):
+        source = shifted(main, row, b, e, cells)
+        wall = walls[k, x]
+        passed[k, x] = jnp.where(wall > 0.5 * BIG, source, collided[step, opposite, x] + wall)
+
+    def passed_middle(step, x):
         for k in range(27):
             if k == 13:
                 continue
             a, b, e = (digit - 1 for digit in digits(k))
-            origin = x - a
             row = None
-            if origin < 0 or origin > last:
-                side = 0 if a == 1 else 1
-                main = get_x[step, side, 3 * (b + 1) + (e + 1)]
+            if b != 0:
+                row = get_y[step, (1 - b) // 2, 9 * (x - a) + 3 * (a + 1) + (e + 1)]
+            passed_on(step, k, x, 26 - k, collided[step, k, x - a], row, b, e)
+
+    def passed_edge(step, side):
+        x = last * side
+        into, back = (18 - 18 * side, 18 * side)
+        inner = x + 1 - 2 * side
+        for b in (-1, 0, 1):
+            turn = (1 - b) // 2
+            for e in (-1, 0, 1):
+                place = 3 * (b + 1) + (e + 1)
+                row = None
                 if b != 0:
-                    if a == 1:
-                        which = RIGHT_UP if b == 1 else RIGHT_DOWN
-                    else:
-                        which = LEFT_UP if b == 1 else LEFT_DOWN
-                    corner = get_d.at[step, which - RIGHT_UP]
-                    row = jnp.concatenate(
-                        [corner[pl.ds(2 * e + 2, 1), :], corner[pl.ds(2 * e + 3, 1), :]], axis=1
+                    row = get_d[step, 2 * side + turn, e + 1]
+                passed_on(
+                    step, into + place, x, back + (8 - place), get_x[step, side, place], row, b, e
+                )
+                if b != 0 or e != 0:
+                    if b != 0:
+                        row = get_y[step, turn, 9 * x + 3 + (e + 1)]
+                    passed_on(
+                        step, 9 + place, x, 17 - place, collided[step, 9 + place, x], row, b, e
                     )
-            else:
-                main = collided[step, k, origin]
                 if b != 0:
-                    place = (3 * (a + 1) + (e + 1)) * depth + origin
-                    row = get_y[step, 0 if b == 1 else 1, pl.ds(place, 1), :]
-            source = shifted(main, row, b, e, cells)
-            wall = walls[k, x]
-            passed[k, x] = jnp.where(wall > 0.5 * BIG, source, collided[step, 26 - k, x] + wall)
+                    row = get_y[step, turn, 9 * inner + 6 * side + (e + 1)]
+                passed_on(
+                    step, back + place, x, into + (8 - place),
+                    collided[step, back + place, inner], row, b, e,
+                )
 
     def field_values(kind, index):
         velocity = [jnp.zeros(kind.shape, jnp.float32) for _ in range(3)]
-        for entry in range(vent_table.shape[0]):
+        for entry in range(vent_table.shape[1]):
             chosen = index == entry
             for axis in range(3):
-                velocity[axis] = jnp.where(chosen, vent_table[entry, axis], velocity[axis])
+                velocity[axis] = jnp.where(chosen, vent_table[axis, entry], velocity[axis])
         is_open = (kind == 0) | (kind >= 3)
         vent = kind == 2
         result = [jnp.where(is_open, BIG, 0.0)]
@@ -291,9 +356,9 @@
     def prepare_walls():
         for plane in range(depth + 2):
             if plane == 0:
-                kind, index = get_kx[RIGHT, 0], get_kx[RIGHT, 1]
+                kind, index = get_kx[0, 0], get_kx[0, 1]
             elif plane == depth + 1:
-                kind, index = get_kx[LEFT, 0], get_kx[LEFT, 1]
+                kind, index = get_kx[1, 0], get_kx[1, 1]
             else:
                 kind, index = kinds[plane - 1], profiles[plane - 1]
             values, velocity = field_values(kind, index)
@@ -302,18 +367,14 @@
             if 1 <= plane <= depth:
                 for axis in range(3):
                     inlet[axis, plane - 1] = jnp.where(kind == 3, velocity[axis], 0.0)
-        for side, b in ((0, 1), (1, -1)):
-            low = (RIGHT_UP if b == 1 else RIGHT_DOWN) - RIGHT_UP
-            high = (LEFT_UP if b == 1 else LEFT_DOWN) - RIGHT_UP
+        for side in range(2):
             for target, shift in ((rim_kinds, 0), (rim_profiles, 1)):
                 target[side] = jnp.zeros((rows, cells), jnp.int32)
-                target[side, pl.ds(1, depth), :] = get_ky[side, pl.ds(shift * depth, depth), :]
-                for row, corner in ((0, low), (depth + 1, high)):
-                    for part in range(2):
-                        target[side, pl.ds(row, 1), pl.ds(part * half, half)] = get_kd[
-                            corner, pl.ds(2 * shift + part, 1), :
-                        ]
-            outside = row_place == (0 if b == 1 else PY - 1)
+                for x in range(depth):
+                    target[side, pl.ds(x + 1, 1), :] = get_ky[side, shift * depth + x]
+                for row, place in ((0, side), (depth + 1, 2 + side)):
+                    target[side, pl.ds(row, 1), :] = get_kd[place, shift]
+            outside = row_place == (0 if side == 0 else PY - 1)
             kind = jnp.where(outside, 1, rim_kinds[side])
             values, _ = field_values(kind, rim_profiles[side])
             for field in range(4):
@@ -344,77 +405,112 @@
 
     for x in order:
         loads[x].wait()
-        by_halves(collide_first, (x,))
-    for which in range(RIGHT_UP, LEFT_UP + 1):
-        stage_diagonal(0, which)
-    stage_rows(0)
+        by_halves(collide_first, x, 1)
+    for side in range(2):
+        stage_corners(0, side)
+        stage_edge(0, side)
+    for x in range(1, last):
+        stage_rows(0, x, range(9))
     kind_load.wait()
     profile_load.wait()
-    for which, x in ((RIGHT, last), (LEFT, 0)):
-        put_kx[which, 0] = kinds[x]
-        put_kx[which, 1] = profiles[x]
-    for side, y in ((0, rows - 1), (1, 0)):
+    for side, x in ((0, last), (1, 0)):
+        put_kx[side, 0] = kinds[x]
+        put_kx[side, 1] = profiles[x]
+        for turn in range(2):
+            y = rows - 1 if turn == 0 else 0
+            put_kd[2 * side + turn, 0] = kinds[x, pl.ds(y, 1), :]
+            put_kd[2 * side + turn, 1] = profiles[x, pl.ds(y, 1), :]
+    for turn in range(2):
+        y = rows - 1 if turn == 0 else 0
         for x in range(depth):
-            put_ky[side, pl.ds(x, 1), :] = kinds[x, pl.ds(y, 1), :]
-            put_ky[side, pl.ds(depth + x, 1), :] = profiles[x, pl.ds(y, 1), :]
-    for which in range(RIGHT_UP, LEFT_UP + 1):
-        x = last if which in (RIGHT_UP, RIGHT_DOWN) else 0
-        y = rows - 1 if which in (RIGHT_UP, LEFT_UP) else 0
-        for shift, source in ((0, kinds), (1, profiles)):
-            row = source[x, pl.ds(y, 1), :]
-            put_kd[which - RIGHT_UP, pl.ds(2 * shift, 1), :] = row[:, :half]
-            put_kd[which - RIGHT_UP, pl.ds(2 * shift + 1, 1), :] = row[:, half:]
-
-    pl.semaphore_wait(barrier, len(targets))
-    for which in range(8):
-        message(0, which).start()
-    for which in range(8):
-        kind_message(which).start()
+            put_ky[turn, x] = kinds[x, pl.ds(y, 1), :]
+            put_ky[turn, depth + x] = profiles[x, pl.ds(y, 1), :]
+
+    far = jnp.where(far_right, 0, 1)
+    sides = (far, 1 - far)
+    pl.semaphore_wait(barrier, 8)
+    for number, side in enumerate(sides):
+        if number == 1:
+            across(0, sides[0]).wait_send()
+        across(0, side).start()
+        for turn in range(2):
+            go(lambda: corner(0, side, turn), turn)
+        kind_across(side).start()
+        for turn in range(2):
+            go(lambda: kind_corner(side, turn), turn)
+        if number == 0:
+            for turn in range(2):
+                go(lambda: along_middle(0, turn), turn)
+                go(lambda: along_edge(0, turn, 0), turn)
+                go(lambda: along_edge(0, turn, 1), turn)
+                go(lambda: kind_along(turn), turn)
 
     outs = []
     for step in range(STEPS):
         final = step == STEPS - 1
         work = finish if final else collide_next
 
-        def advance(planes):
-            for x in planes:
-                passed_plane(step, x)
-            by_halves(lambda x, lanes: work(step, x, lanes), planes)
+        def write(x, number):
+            copy = pltpu.make_async_copy(start.at[:, x], out.at[:, 0, x], out_sem.at[number])
+            copy.start()
+            outs.append(copy)
+
+        if step == 0:
+            for side in range(2):
+                kind_across(side).wait_recv()
+                for turn in range(2):
+                    came(lambda: kind_corner(side, turn), turn)
+            for turn in range(2):
+                came(lambda: kind_along(turn), turn)
+            prepare_walls()
+        for turn in range(2):
+            came(lambda: along_middle(step, turn), turn)
+            for side in range(2):
+                came(lambda: along_edge(step, turn, side), turn)
+        for x in range(1, last):
+            passed_middle(step, x)
+        by_halves(lambda x, lanes: work(step, x, lanes), 1, last - 1)
+        if final:
+            for x in range(1, last):
+                write(x, x)
+        else:
+            for x in range(1, last):
+                stage_rows(step + 1, x, range(9))
+            for turn in range(2):
+                go(lambda: along_middle(step + 1, turn), turn)
+        for number, side in enumerate(sides):
+            across(step, 1 - side).wait_recv()
+            for turn in range(2):
+                came(lambda: corner(step, 1 - side, turn), turn)
+            passed_edge(step, 1 - side)
+            x = last - last * side
+            by_halves(lambda x, lanes: work(step, x, lanes), x, 1)
             if final:
-                for x in planes:
-                    copy = pltpu.make_async_copy(start.at[:, x], out.at[:, 0, x], out_sem.at[x])
-                    copy.start()
-                    outs.append(copy)
-
-        if step == 0:
-            for which in range(8):
-                kind_message(which).wait_recv()
-            prepare_walls()
-        for which in (UP, DOWN):
-            message(step, which).wait_recv()
-        advance(tuple(range(1, last)))
-        for x, needed, sent in (
-            (0, (RIGHT, RIGHT_UP, RIGHT_DOWN), (LEFT, LEFT_DOWN, LEFT_UP)),
-            (last, (LEFT, LEFT_DOWN, LEFT_UP), (RIGHT, RIGHT_UP, RIGHT_DOWN)),
-        ):
-            for which in needed:
-                message(step, which).wait_recv()
-            advance((x,))
-            if not final:
-                message(step + 1, sent[0]).start()
-                for which in sent[1:]:
-                    stage_diagonal(step + 1, which)
-                    message(step + 1, which).start()
-        if not final:
-            stage_rows(step + 1)
-            for which in (UP, DOWN):
-                message(step + 1, which).start()
+                write(x, last * number)
+            else:
+                across(step + 1, side).start()
+                stage_corners(step + 1, side)
+                for turn in range(2):
+                    go(lambda: corner(step + 1, side, turn), turn)
+                stage_edge(step + 1, side)
+                for turn in range(2):
+                    go(lambda: along_edge(step + 1, turn, side), turn)
 
     for step in range(STEPS):
-        for which in range(8):
-            message(step, which).wait_send()
-    for which in range(8):
-        kind_message(which).wait_send()
+        for number, side in enumerate(sides):
+            if step > 0 or number == 1:
+                across(step, side).wait_send()
+            for turn in range(2):
+                sent(lambda: corner(step, side, turn), turn)
+                sent(lambda: along_edge(step, turn, side), turn)
+        for turn in range(2):
+            sent(lambda: along_middle(step, turn), turn)
+    for side in range(2):
+        kind_across(side).wait_send()
+        for turn in range(2):
+            sent(lambda: kind_corner(side, turn), turn)
+    for turn in range(2):
+        sent(lambda: kind_along(turn), turn)
     for copy in outs:
         copy.wait()
 
@@ -422,7 +518,7 @@
 def local(populations, cell_kind, profile, vent_table, rates):
     _, _, depth, rows, cells = populations.shape
     half = cells // 2
-    strip = (9 * depth + 7) // 8 * 8
+    strip = 9 * depth
     f32, i32 = jnp.float32, jnp.int32
     anywhere = pl.BlockSpec(memory_space=pl.ANY)
     scalar = pl.BlockSpec(memory_space=pltpu.SMEM)
@@ -445,24 +541,24 @@
             pltpu.VMEM((4, depth + 2, rows, cells), f32),
             pltpu.VMEM((2, 4, rows, cells), f32),
             pltpu.VMEM((STEPS, 2, 9, rows, cells), f32),
-            pltpu.VMEM((STEPS, 2, strip, cells), f32),
-            pltpu.VMEM((STEPS, 2, strip, cells), f32),
-            pltpu.VMEM((STEPS, 4, 8, half), f32),
-            pltpu.VMEM((STEPS, 4, 8, half), f32),
+            pltpu.VMEM((STEPS, 2, strip, 1, cells), f32),
+            pltpu.VMEM((STEPS, 2, strip, 1, cells), f32),
+            pltpu.VMEM((STEPS, 4, 3, 1, cells), f32),
+            pltpu.VMEM((STEPS, 4, 3, 1, cells), f32),
             pltpu.VMEM((2, 2, rows, cells), i32),
             pltpu.VMEM((2, 2, rows, cells), i32),
-            pltpu.VMEM((2, 2 * depth, cells), i32),
-            pltpu.VMEM((2, 2 * depth, cells), i32),
-            pltpu.VMEM((4, 8, half), i32),
-            pltpu.VMEM((4, 8, half), i32),
+            pltpu.VMEM((2, 2 * depth, 1, cells), i32),
+            pltpu.VMEM((2, 2 * depth, 1, cells), i32),
+            pltpu.VMEM((4, 2, 1, cells), i32),
+            pltpu.VMEM((4, 2, 1, cells), i32),
             pltpu.SemaphoreType.DMA((depth + 2,)),
             pltpu.SemaphoreType.DMA((depth,)),
-            pltpu.SemaphoreType.DMA((STEPS + 1, 8)),
-            pltpu.SemaphoreType.DMA((STEPS + 1, 8)),
+            pltpu.SemaphoreType.DMA((STEPS + 1, ROW)),
+            pltpu.SemaphoreType.DMA((STEPS + 1, ROW)),
         ],
         compiler_params=pltpu.CompilerParams(collective_id=0, has_side_effects=True),
         name="lattice_steps",
-    )(populations, cell_kind, profile, vent_table, rates)
+    )(populations, cell_kind, profile, vent_table.T, rates)
 
 
 def solution(mesh):

time: 64.9 us -> 61.8 us (0.952)
  Pallas kernels: 61.1 us -> 59.5 us
  local copies, waits for them, and re-layouts: 3.52 us -> 2.17 us
    pallas_call x1, Pallas kernels: 61.1 us -> 59.5 us  [local(): pl.pallas_call(kernel, out_shape=jax.ShapeDtypeStruct(populations.shape,...]
    unnamed x2 -> x1, local copies, waits for them, and re-layouts: 3.52 us -> 2.17 us
where the time goes in v1:
time: 61.8 us; the launch traced here: 61.6 us
  Pallas kernels  59.5 us (96%)
  local copies, waits for them, and re-layouts  2.17 us (4%)
    pallas_call x1, Pallas kernels, local(): pl.pallas_call(kernel, out_shape=jax.ShapeDtypeStruct(populations.shape,...  59.5 us
    unnamed x1, local copies, waits for them, and re-layouts  2.17 us

profile of v1, /device:TPU:513, one launch (start us, length us, event | category | flops | bytes accessed | tf_op | source)
XLA Modules:
  0.0 61.6 jit_solution(48887533275558771)
XLA Ops:
  0.0 59.5 %lattice_steps.1 = f32[27,1,4,8,256]{4,3,2,1,0:T(8,128)} custom-call(f32[27,1,4,8,256]{4,3,2,1,0:T(8,128)} %populations.1, s32[1,4,8,256]{3,2,1,0:T(8,128)} %cell_kind.1, s32[1,4,8,256]{3,2,1,0:T(8,128)} %profile.1, f32[3,8]{1,0:T(4,128)} %bitcast.1, f32[27]{0:T(128)} %rates.1), custom_call_target="tpu_custom_call" | custom-call | tf_op jit(solution)/shard_map/lattice_steps/pallas_call | solution.py:525
  59.5 2.2 %copy.7 = f32[27,1,4,8,256]{4,3,2,1,0:T(8,128)} copy(f32[27,1,4,8,256]{4,3,2,1,0:T(8,128)} %lattice_steps.1) | data formatting | bytes 1769472

commit v2 on v1

--- a/solution.py
+++ b/solution.py
@@ -429,21 +429,31 @@
     far = jnp.where(far_right, 0, 1)
     sides = (far, 1 - far)
     pl.semaphore_wait(barrier, 8)
+    for side in sides:
+        kind_across(side).start()
+        for turn in range(2):
+            go(lambda: kind_corner(side, turn), turn)
+    for turn in range(2):
+        go(lambda: kind_along(turn), turn)
     for number, side in enumerate(sides):
         if number == 1:
             across(0, sides[0]).wait_send()
+        for turn in range(2):
+            go(lambda: corner(0, side, turn), turn)
         across(0, side).start()
-        for turn in range(2):
-            go(lambda: corner(0, side, turn), turn)
-        kind_across(side).start()
-        for turn in range(2):
-            go(lambda: kind_corner(side, turn), turn)
         if number == 0:
             for turn in range(2):
                 go(lambda: along_middle(0, turn), turn)
-                go(lambda: along_edge(0, turn, 0), turn)
-                go(lambda: along_edge(0, turn, 1), turn)
-                go(lambda: kind_along(turn), turn)
+                go(lambda: along_edge(0, turn, sides[0]), turn)
+                go(lambda: along_edge(0, turn, sides[1]), turn)
+
+    for side in sides:
+        kind_across(side).wait_recv()
+        for turn in range(2):
+            came(lambda: kind_corner(side, turn), turn)
+    for turn in range(2):
+        came(lambda: kind_along(turn), turn)
+    prepare_walls()
 
     outs = []
     for step in range(STEPS):
@@ -455,18 +465,31 @@
             copy.start()
             outs.append(copy)
 
-        if step == 0:
-            for side in range(2):
-                kind_across(side).wait_recv()
+        def edge(number):
+            side = sides[number]
+            across(step, 1 - side).wait_recv()
+            for turn in range(2):
+                came(lambda: corner(step, 1 - side, turn), turn)
+            passed_edge(step, 1 - side)
+            x = last - last * side
+            by_halves(lambda x, lanes: work(step, x, lanes), x, 1)
+            if final:
+                write(x, last * number)
+            else:
+                stage_corners(step + 1, side)
                 for turn in range(2):
-                    came(lambda: kind_corner(side, turn), turn)
-            for turn in range(2):
-                came(lambda: kind_along(turn), turn)
-            prepare_walls()
+                    go(lambda: corner(step + 1, side, turn), turn)
+                stage_edge(step + 1, side)
+                for turn in range(2):
+                    go(lambda: along_edge(step + 1, turn, side), turn)
+                across(step + 1, side).start()
+
         for turn in range(2):
             came(lambda: along_middle(step, turn), turn)
-            for side in range(2):
-                came(lambda: along_edge(step, turn, side), turn)
+            came(lambda: along_edge(step, turn, sides[0]), turn)
+        edge(0)
+        for turn in range(2):
+            came(lambda: along_edge(step, turn, sides[1]), turn)
         for x in range(1, last):
             passed_middle(step, x)
         by_halves(lambda x, lanes: work(step, x, lanes), 1, last - 1)
@@ -478,23 +501,7 @@
                 stage_rows(step + 1, x, range(9))
             for turn in range(2):
                 go(lambda: along_middle(step + 1, turn), turn)
-        for number, side in enumerate(sides):
-            across(step, 1 - side).wait_recv()
-            for turn in range(2):
-                came(lambda: corner(step, 1 - side, turn), turn)
-            passed_edge(step, 1 - side)
-            x = last - last * side
-            by_halves(lambda x, lanes: work(step, x, lanes), x, 1)
-            if final:
-                write(x, last * number)
-            else:
-                across(step + 1, side).start()
-                stage_corners(step + 1, side)
-                for turn in range(2):
-                    go(lambda: corner(step + 1, side, turn), turn)
-                stage_edge(step + 1, side)
-                for turn in range(2):
-                    go(lambda: along_edge(step + 1, turn, side), turn)
+        edge(1)
 
     for step in range(STEPS):
         for number, side in enumerate(sides):

time: 61.8 us -> 53.4 us (0.86)
  Pallas kernels: 59.5 us -> 51.1 us
    pallas_call x1, Pallas kernels: 59.5 us -> 51.1 us  [local(): pl.pallas_call(kernel, out_shape=jax.ShapeDtypeStruct(populations.shape,...]
where the time goes in v2:
time: 53.4 us; the launch traced here: 53.2 us
  Pallas kernels  51.1 us (96%)
  local copies, waits for them, and re-layouts  2.17 us (4%)
    pallas_call x1, Pallas kernels, local(): pl.pallas_call(kernel, out_shape=jax.ShapeDtypeStruct(populations.shape,...  51.1 us
    unnamed x1, local copies, waits for them, and re-layouts  2.17 us

profile of v2, /device:TPU:513, one launch (start us, length us, event | category | flops | bytes accessed | tf_op | source)
XLA Modules:
  0.0 53.2 jit_solution(15298456114148656112)
XLA Ops:
  0.0 51.1 %lattice_steps.1 = f32[27,1,4,8,256]{4,3,2,1,0:T(8,128)} custom-call(f32[27,1,4,8,256]{4,3,2,1,0:T(8,128)} %populations.1, s32[1,4,8,256]{3,2,1,0:T(8,128)} %cell_kind.1, s32[1,4,8,256]{3,2,1,0:T(8,128)} %profile.1, f32[3,8]{1,0:T(4,128)} %bitcast.1, f32[27]{0:T(128)} %rates.1), custom_call_target="tpu_custom_call" | custom-call | tf_op jit(solution)/shard_map/lattice_steps/pallas_call | solution.py:532
  51.1 2.2 %copy.7 = f32[27,1,4,8,256]{4,3,2,1,0:T(8,128)} copy(f32[27,1,4,8,256]{4,3,2,1,0:T(8,128)} %lattice_steps.1) | data formatting | bytes 1769472

commit v3 on v2

--- a/solution.py
+++ b/solution.py
@@ -107,7 +107,7 @@
     rim_kinds, rim_profiles, fields, rim_fields,
     get_x, put_y, get_y, put_d, get_d,
     put_kx, get_kx, put_ky, get_ky, put_kd, get_kd,
-    load_sem, out_sem, send_sem, recv_sem,
+    load_sem, send_sem, recv_sem,
 ):
     me = lax.axis_index("gx")
     count = lax.axis_size("gx")
@@ -115,7 +115,7 @@
     last = depth - 1
     half = cells // 2
     row_place = lax.rem(me + PY // 2, PY)
-    far_right = lax.rem(me // PY, 2) == 1
+    right_first = lax.rem((me + PY // 2) // PY, 2) == 1
     has_row = (row_place != PY - 1, row_place != 0)
 
     def device(side, turn):
@@ -263,7 +263,7 @@
         ]
         forced = equilibrium(velocity)
         for k in range(27):
-            start[k, x, :, lanes] = jnp.where(fluid, values[k], forced[k])
+            out[k, 0, x, :, lanes] = jnp.where(fluid, values[k], forced[k])
 
     def by_halves(work, first, planes):
         def body(index, carry):
@@ -426,8 +426,8 @@
             put_ky[turn, x] = kinds[x, pl.ds(y, 1), :]
             put_ky[turn, depth + x] = profiles[x, pl.ds(y, 1), :]
 
-    far = jnp.where(far_right, 0, 1)
-    sides = (far, 1 - far)
+    early = jnp.where(right_first, 0, 1)
+    sides = (early, 1 - early)
     pl.semaphore_wait(barrier, 8)
     for side in sides:
         kind_across(side).start()
@@ -455,15 +455,9 @@
         came(lambda: kind_along(turn), turn)
     prepare_walls()
 
-    outs = []
     for step in range(STEPS):
         final = step == STEPS - 1
         work = finish if final else collide_next
-
-        def write(x, number):
-            copy = pltpu.make_async_copy(start.at[:, x], out.at[:, 0, x], out_sem.at[number])
-            copy.start()
-            outs.append(copy)
 
         def edge(number):
             side = sides[number]
@@ -473,9 +467,7 @@
             passed_edge(step, 1 - side)
             x = last - last * side
             by_halves(lambda x, lanes: work(step, x, lanes), x, 1)
-            if final:
-                write(x, last * number)
-            else:
+            if not final:
                 stage_corners(step + 1, side)
                 for turn in range(2):
                     go(lambda: corner(step + 1, side, turn), turn)
@@ -493,10 +485,7 @@
         for x in range(1, last):
             passed_middle(step, x)
         by_halves(lambda x, lanes: work(step, x, lanes), 1, last - 1)
-        if final:
-            for x in range(1, last):
-                write(x, x)
-        else:
+        if not final:
             for x in range(1, last):
                 stage_rows(step + 1, x, range(9))
             for turn in range(2):
@@ -518,8 +507,6 @@
             sent(lambda: kind_corner(side, turn), turn)
     for turn in range(2):
         sent(lambda: kind_along(turn), turn)
-    for copy in outs:
-        copy.wait()
 
 
 def local(populations, cell_kind, profile, vent_table, rates):
@@ -531,9 +518,9 @@
     scalar = pl.BlockSpec(memory_space=pltpu.SMEM)
     return pl.pallas_call(
         kernel,
-        out_shape=jax.ShapeDtypeStruct(populations.shape, f32),
+        out_shape=pltpu.VMEM(populations.shape, f32),
         in_specs=[anywhere, anywhere, anywhere, scalar, scalar],
-        out_specs=anywhere,
+        out_specs=pl.BlockSpec(memory_space=pltpu.VMEM),
         scratch_shapes=[
             pltpu.VMEM((27, depth, rows, cells), f32),
             pltpu.VMEM((STEPS, 27, depth, rows, cells), f32),
@@ -559,7 +546,6 @@
             pltpu.VMEM((4, 2, 1, cells), i32),
             pltpu.VMEM((4, 2, 1, cells), i32),
             pltpu.SemaphoreType.DMA((depth + 2,)),
-            pltpu.SemaphoreType.DMA((depth,)),
             pltpu.SemaphoreType.DMA((STEPS + 1, ROW)),
             pltpu.SemaphoreType.DMA((STEPS + 1, ROW)),
         ],

time: 53.4 us -> 50.4 us (0.944)
  Pallas kernels: 51.1 us -> 49.4 us
  local copies, waits for them, and re-layouts: 2.17 us -> 0.91 us
    pallas_call x1, Pallas kernels: 51.1 us -> 49.4 us  [local(): pl.pallas_call(kernel, out_shape=pltpu.VMEM(populations.shape, f32), in_s...]
    unnamed x1, local copies, waits for them, and re-layouts: 2.17 us -> 0.91 us
where the time goes in v3:
time: 50.4 us; the launch traced here: 50.3 us
  Pallas kernels  49.4 us (98%)
  local copies, waits for them, and re-layouts  0.91 us (2%)
    pallas_call x1, Pallas kernels, local(): pl.pallas_call(kernel, out_shape=pltpu.VMEM(populations.shape, f32), in_s...  49.4 us

profile of v3, /device:TPU:513, one launch (start us, length us, event | category | flops | bytes accessed | tf_op | source)
XLA Modules:
  0.0 50.3 jit_solution(8215626334101663963)
XLA Ops:
  0.0 49.4 %lattice_steps.1 = f32[27,1,4,8,256]{4,3,2,1,0:T(8,128)S(1)} custom-call(f32[27,1,4,8,256]{4,3,2,1,0:T(8,128)} %populations.1, s32[1,4,8,256]{3,2,1,0:T(8,128)} %cell_kind.1, s32[1,4,8,256]{3,2,1,0:T(8,128)} %profile.1, f32[3,8]{1,0:T(4,128)} %bitcast.1, f32[27]{0:T(128)} %rates.1), custom_call_target="tpu_custom_call" | custom-call | tf_op jit(solution)/shard_map/lattice_steps/pallas_call | solution.py:519
  49.4 0.9 %copy.7 = f32[27,1,4,8,256]{4,3,2,1,0:T(8,128)} copy(f32[27,1,4,8,256]{4,3,2,1,0:T(8,128)S(1)} %lattice_steps.1) | data formatting | bytes 1769472

commit v4 on v3

--- a/solution.py
+++ b/solution.py
@@ -157,6 +157,12 @@
     def across(step, side):
         source = collided.at[step, pl.ds(18 - 18 * side, 9), last - last * side]
         return remote(source, get_x.at[step, side], step, ACROSS + side, side, None)
+
+    def across_go(step, side):
+        for first in range(0, 9, 1):
+            source = collided.at[step, pl.ds(18 - 18 * side + first, 1), last - last * side]
+            target = get_x.at[step, side, pl.ds(first, 1)]
+            remote(source, target, step, ACROSS + side, side, None).start()
 
     def corner(step, side, turn):
         place = 2 * side + turn
@@ -440,7 +446,7 @@
             across(0, sides[0]).wait_send()
         for turn in range(2):
             go(lambda: corner(0, side, turn), turn)
-        across(0, side).start()
+        across_go(0, side)
         if number == 0:
             for turn in range(2):
                 go(lambda: along_middle(0, turn), turn)
@@ -455,9 +461,28 @@
         came(lambda: kind_along(turn), turn)
     prepare_walls()
 
+    def all_sent(step):
+        for number, side in enumerate(sides):
+            if step > 0 or number == 1:
+                across(step, side).wait_send()
+            for turn in range(2):
+                sent(lambda: corner(step, side, turn), turn)
+                sent(lambda: along_edge(step, turn, side), turn)
+        for turn in range(2):
+            sent(lambda: along_middle(step, turn), turn)
+
     for step in range(STEPS):
         final = step == STEPS - 1
         work = finish if final else collide_next
+        if final:
+            for earlier in range(step):
+                all_sent(earlier)
+            for side in range(2):
+                kind_across(side).wait_send()
+                for turn in range(2):
+                    sent(lambda: kind_corner(side, turn), turn)
+            for turn in range(2):
+                sent(lambda: kind_along(turn), turn)
 
         def edge(number):
             side = sides[number]
@@ -474,7 +499,7 @@
                 stage_edge(step + 1, side)
                 for turn in range(2):
                     go(lambda: along_edge(step + 1, turn, side), turn)
-                across(step + 1, side).start()
+                across_go(step + 1, side)
 
         for turn in range(2):
             came(lambda: along_middle(step, turn), turn)
@@ -492,21 +517,7 @@
                 go(lambda: along_middle(step + 1, turn), turn)
         edge(1)
 
-    for step in range(STEPS):
-        for number, side in enumerate(sides):
-            if step > 0 or number == 1:
-                across(step, side).wait_send()
-            for turn in range(2):
-                sent(lambda: corner(step, side, turn), turn)
-                sent(lambda: along_edge(step, turn, side), turn)
-        for turn in range(2):
-            sent(lambda: along_middle(step, turn), turn)
-    for side in range(2):
-        kind_across(side).wait_send()
-        for turn in range(2):
-            sent(lambda: kind_corner(side, turn), turn)
-    for turn in range(2):
-        sent(lambda: kind_along(turn), turn)
+    all_sent(STEPS - 1)
 
 
 def local(populations, cell_kind, profile, vent_table, rates):

time: 50.4 us -> 50.1 us (level)
  no operation moved by 1% of the time
where the time goes in v4:
time: 50.1 us; the launch traced here: 49.9 us
  Pallas kernels  49 us (98%)
  local copies, waits for them, and re-layouts  0.91 us (2%)
    pallas_call x1, Pallas kernels, local(): pl.pallas_call(kernel, out_shape=pltpu.VMEM(populations.shape, f32), in_s...  49 us

profile of v4, /device:TPU:513, one launch (start us, length us, event | category | flops | bytes accessed | tf_op | source)
XLA Modules:
  0.0 49.9 jit_solution(10580803019676328347)
XLA Ops:
  0.0 49.0 %lattice_steps.1 = f32[27,1,4,8,256]{4,3,2,1,0:T(8,128)S(1)} custom-call(f32[27,1,4,8,256]{4,3,2,1,0:T(8,128)} %populations.1, s32[1,4,8,256]{3,2,1,0:T(8,128)} %cell_kind.1, s32[1,4,8,256]{3,2,1,0:T(8,128)} %profile.1, f32[3,8]{1,0:T(4,128)} %bitcast.1, f32[27]{0:T(128)} %rates.1), custom_call_target="tpu_custom_call" | custom-call | tf_op jit(solution)/shard_map/lattice_steps/pallas_call | solution.py:530
  49.0 0.9 %copy.7 = f32[27,1,4,8,256]{4,3,2,1,0:T(8,128)} copy(f32[27,1,4,8,256]{4,3,2,1,0:T(8,128)S(1)} %lattice_steps.1) | data formatting | bytes 1769472

commit v5 on v4

--- a/solution.py
+++ b/solution.py
@@ -319,7 +319,7 @@
                 row = get_y[step, (1 - b) // 2, 9 * (x - a) + 3 * (a + 1) + (e + 1)]
             passed_on(step, k, x, 26 - k, collided[step, k, x - a], row, b, e)
 
-    def passed_edge(step, side):
+    def passed_edge_own(step, side):
         x = last * side
         into, back = (18 - 18 * side, 18 * side)
         inner = x + 1 - 2 * side
@@ -328,11 +328,6 @@
             for e in (-1, 0, 1):
                 place = 3 * (b + 1) + (e + 1)
                 row = None
-                if b != 0:
-                    row = get_d[step, 2 * side + turn, e + 1]
-                passed_on(
-                    step, into + place, x, back + (8 - place), get_x[step, side, place], row, b, e
-                )
                 if b != 0 or e != 0:
                     if b != 0:
                         row = get_y[step, turn, 9 * x + 3 + (e + 1)]
@@ -346,6 +341,20 @@
                     collided[step, back + place, inner], row, b, e,
                 )
 
+    def passed_edge(step, side):
+        x = last * side
+        into, back = (18 - 18 * side, 18 * side)
+        for b in (-1, 0, 1):
+            turn = (1 - b) // 2
+            for e in (-1, 0, 1):
+                place = 3 * (b + 1) + (e + 1)
+                row = None
+                if b != 0:
+                    row = get_d[step, 2 * side + turn, e + 1]
+                passed_on(
+                    step, into + place, x, back + (8 - place), get_x[step, side, place], row, b, e
+                )
+
     def field_values(kind, index):
         velocity = [jnp.zeros(kind.shape, jnp.float32) for _ in range(3)]
         for entry in range(vent_table.shape[1]):
@@ -359,20 +368,19 @@
             result.append(jnp.where(vent, velocity[axis], 0.0))
         return result, velocity
 
+    def prepare_fields():
+        for x in range(depth):
+            values, velocity = field_values(kinds[x], profiles[x])
+            for field in range(4):
+                fields[field, x + 1] = values[field]
+            for axis in range(3):
+                inlet[axis, x] = jnp.where(kinds[x] == 3, velocity[axis], 0.0)
+
     def prepare_walls():
-        for plane in range(depth + 2):
-            if plane == 0:
-                kind, index = get_kx[0, 0], get_kx[0, 1]
-            elif plane == depth + 1:
-                kind, index = get_kx[1, 0], get_kx[1, 1]
-            else:
-                kind, index = kinds[plane - 1], profiles[plane - 1]
-            values, velocity = field_values(kind, index)
+        for plane, side in ((0, 0), (depth + 1, 1)):
+            values, _ = field_values(get_kx[side, 0], get_kx[side, 1])
             for field in range(4):
                 fields[field, plane] = values[field]
-            if 1 <= plane <= depth:
-                for axis in range(3):
-                    inlet[axis, plane - 1] = jnp.where(kind == 3, velocity[axis], 0.0)
         for side in range(2):
             for target, shift in ((rim_kinds, 0), (rim_profiles, 1)):
                 target[side] = jnp.zeros((rows, cells), jnp.int32)
@@ -453,6 +461,7 @@
                 go(lambda: along_edge(0, turn, sides[0]), turn)
                 go(lambda: along_edge(0, turn, sides[1]), turn)
 
+    prepare_fields()
     for side in sides:
         kind_across(side).wait_recv()
         for turn in range(2):
@@ -486,6 +495,7 @@
 
         def edge(number):
             side = sides[number]
+            passed_edge_own(step, 1 - side)
             across(step, 1 - side).wait_recv()
             for turn in range(2):
                 came(lambda: corner(step, 1 - side, turn), turn)

time: 50.1 us -> 49.9 us (level)
  no operation moved by 1% of the time
where the time goes in v5:
time: 49.9 us; the launch traced here: 49.8 us
  Pallas kernels  48.9 us (98%)
  local copies, waits for them, and re-layouts  0.91 us (2%)
    pallas_call x1, Pallas kernels, local(): pl.pallas_call(kernel, out_shape=pltpu.VMEM(populations.shape, f32), in_s...  48.9 us

profile of v5, /device:TPU:513, one launch (start us, length us, event | category | flops | bytes accessed | tf_op | source)
XLA Modules:
  0.0 49.8 jit_solution(17808793109980169066)
XLA Ops:
  0.0 48.9 %lattice_steps.1 = f32[27,1,4,8,256]{4,3,2,1,0:T(8,128)S(1)} custom-call(f32[27,1,4,8,256]{4,3,2,1,0:T(8,128)} %populations.1, s32[1,4,8,256]{3,2,1,0:T(8,128)} %cell_kind.1, s32[1,4,8,256]{3,2,1,0:T(8,128)} %profile.1, f32[3,8]{1,0:T(4,128)} %bitcast.1, f32[27]{0:T(128)} %rates.1), custom_call_target="tpu_custom_call" | custom-call | tf_op jit(solution)/shard_map/lattice_steps/pallas_call | solution.py:540
  48.9 0.9 %copy.7 = f32[27,1,4,8,256]{4,3,2,1,0:T(8,128)} copy(f32[27,1,4,8,256]{4,3,2,1,0:T(8,128)S(1)} %lattice_steps.1) | data formatting | bytes 1769472

commit v6 on v5

--- a/solution.py
+++ b/solution.py
@@ -368,6 +368,29 @@
             result.append(jnp.where(vent, velocity[axis], 0.0))
         return result, velocity
 
+    def wall_part(plane, b):
+        lane = lax.broadcasted_iota(jnp.int32, (rows, cells), 1)
+        for e in (-1, 0, 1):
+            moved = []
+            for field in range(4):
+                row = None
+                if b != 0:
+                    row = rim_fields[0 if b == 1 else 1, field, pl.ds(plane, 1), :]
+                value = shifted(fields[field, plane], row, b, e, cells)
+                if e != 0:
+                    value = jnp.where(lane == (0 if e == 1 else cells - 1), 0.0, value)
+                moved.append(value)
+            cross = moved[0]
+            if b != 0:
+                cross = cross + (6.0 * b) * moved[2]
+            if e != 0:
+                cross = cross + (6.0 * e) * moved[3]
+            for a in (-1, 0, 1):
+                x = plane - 1 + a
+                k = direction(a, b, e)
+                if 0 <= x <= last and k != 13:
+                    walls[k, x] = cross if a == 0 else cross + (6.0 * a) * moved[1]
+
     def prepare_fields():
         for x in range(depth):
             values, velocity = field_values(kinds[x], profiles[x])
@@ -393,29 +416,10 @@
             values, _ = field_values(kind, rim_profiles[side])
             for field in range(4):
                 rim_fields[side, field] = values[field]
-        lane = lax.broadcasted_iota(jnp.int32, (rows, cells), 1)
         for plane in range(depth + 2):
             for b in (-1, 0, 1):
-                for e in (-1, 0, 1):
-                    moved = []
-                    for field in range(4):
-                        row = None
-                        if b != 0:
-                            row = rim_fields[0 if b == 1 else 1, field, pl.ds(plane, 1), :]
-                        value = shifted(fields[field, plane], row, b, e, cells)
-                        if e != 0:
-                            value = jnp.where(lane == (0 if e == 1 else cells - 1), 0.0, value)
-                        moved.append(value)
-                    cross = moved[0]
-                    if b != 0:
-                        cross = cross + (6.0 * b) * moved[2]
-                    if e != 0:
-                        cross = cross + (6.0 * e) * moved[3]
-                    for a in (-1, 0, 1):
-                        x = plane - 1 + a
-                        k = direction(a, b, e)
-                        if 0 <= x <= last and k != 13:
-                            walls[k, x] = cross if a == 0 else cross + (6.0 * a) * moved[1]
+                if b != 0 or plane in (0, depth + 1):
+                    wall_part(plane, b)
 
     for x in order:
         loads[x].wait()
@@ -462,6 +466,8 @@
                 go(lambda: along_edge(0, turn, sides[1]), turn)
 
     prepare_fields()
+    for plane in range(1, depth + 1):
+        wall_part(plane, 0)
     for side in sides:
         kind_across(side).wait_recv()
         for turn in range(2):

time: 49.9 us -> 49.9 us (level)
  no operation moved by 1% of the time
where the time goes in v6:
time: 49.9 us; the launch traced here: 49.8 us
  Pallas kernels  48.9 us (98%)
  local copies, waits for them, and re-layouts  0.91 us (2%)
    pallas_call x1, Pallas kernels, local(): pl.pallas_call(kernel, out_shape=pltpu.VMEM(populations.shape, f32), in_s...  48.9 us

profile of v6, /device:TPU:513, one launch (start us, length us, event | category | flops | bytes accessed | tf_op | source)
XLA Modules:
  0.0 49.8 jit_solution(2064312609250030184)
XLA Ops:
  0.0 48.9 %lattice_steps.1 = f32[27,1,4,8,256]{4,3,2,1,0:T(8,128)S(1)} custom-call(f32[27,1,4,8,256]{4,3,2,1,0:T(8,128)} %populations.1, s32[1,4,8,256]{3,2,1,0:T(8,128)} %cell_kind.1, s32[1,4,8,256]{3,2,1,0:T(8,128)} %profile.1, f32[3,8]{1,0:T(4,128)} %bitcast.1, f32[27]{0:T(128)} %rates.1), custom_call_target="tpu_custom_call" | custom-call | tf_op jit(solution)/shard_map/lattice_steps/pallas_call | solution.py:546
  48.9 0.9 %copy.7 = f32[27,1,4,8,256]{4,3,2,1,0:T(8,128)} copy(f32[27,1,4,8,256]{4,3,2,1,0:T(8,128)S(1)} %lattice_steps.1) | data formatting | bytes 1769472
